TPU v7x, 32 devices: a whole 2x2x4 slice. The times are simulated.
32 devices in a mesh: dp: 32 (over z, y, x, core).
Axes of the slice: x: 2, y: 2, z: 4, core: 2. Of those that a mesh axis runs over, the one named last changes fastest.
Arguments:
- weights: float32 [790528], P('dp')
- moment_one: float32 [790528], P('dp')
- moment_two: float32 [790528], P('dp')
- x_qkv: bfloat16 [131072, 256], P('dp')
- dy_qkv: bfloat16 [131072, 768], P('dp')
- x_proj: bfloat16 [131072, 256], P('dp')
- dy_proj: bfloat16 [131072, 256], P('dp')
- x_inter: bfloat16 [131072, 256], P('dp')
- dy_inter: bfloat16 [131072, 1024], P('dp')
- x_out: bfloat16 [131072, 1024], P('dp')
- dy_out: bfloat16 [131072, 256], P('dp')
- ln_grad: float32 [32, 4, 256], P('dp')
Outputs:
- output 1: float32 [790528], P('dp')
- output 2: float32 [790528], P('dp')
- output 3: float32 [790528], P('dp')
- output 4: bfloat16 [790528], replicated
All inputs are finite; a program needn't handle non-finite values.
Results may differ from a plain program's by a relative error of at most 0.001.
Values sent between devices are 32-bit elements.
A program may use at most 1 GiB of HBM per device.

v0:
```python
import jax
import jax.numpy as jnp
from jax import lax
from jax.sharding import PartitionSpec as P

STEP = 10
LEARN_RATE = 0.5
BETA_ONE = 0.9
BETA_TWO = 0.999
EPSILON = 1e-6
DECAY = 0.01
NUM_SEGS = 13
CORR_ONE = 1.0 - BETA_ONE ** STEP
CORR_TWO = 1.0 - BETA_TWO ** STEP
CONTRACT_ROWS = (((0,), (0,)), ((), ()))


def tensor_sizes(layer_width):
    return [3 * layer_width * layer_width, 3 * layer_width, layer_width * layer_width, layer_width, layer_width, layer_width,
            4 * layer_width * layer_width, 4 * layer_width, 4 * layer_width * layer_width, layer_width, layer_width, layer_width]


def segment_index(positions, layer_width):
    seg_ids = jnp.zeros(positions.shape, jnp.int32)
    running_end = 0
    for tensor_size in tensor_sizes(layer_width):
        running_end = running_end + tensor_size
        seg_ids = seg_ids + (positions >= running_end).astype(jnp.int32)
    return seg_ids


def tensor_sums(values, seg_ids):
    seg_range = jnp.arange(NUM_SEGS, dtype=jnp.int32)[:, None]
    return jnp.sum(jnp.where(seg_ids[None, :] == seg_range, values[None, :], 0.0), axis=1)


def per_element(table, seg_ids):
    seg_range = jnp.arange(NUM_SEGS, dtype=jnp.int32)[:, None]
    return jnp.sum(jnp.where(seg_ids[None, :] == seg_range, table[:, None], 0.0), axis=0)


def weight_grad(x_rows, dy_rows):
    return lax.dot_general(x_rows, dy_rows, CONTRACT_ROWS, preferred_element_type=jnp.float32)


def bias_grad(dy_rows):
    return jnp.sum(dy_rows, axis=0, dtype=jnp.float32)


def flat_grad(act_pairs, ln_rows, total_len):
    x_qkv, dy_qkv, x_proj, dy_proj, x_inter, dy_inter, x_out, dy_out = act_pairs
    pieces = [weight_grad(x_qkv, dy_qkv), bias_grad(dy_qkv), weight_grad(x_proj, dy_proj), bias_grad(dy_proj),
              ln_rows[0], ln_rows[1], weight_grad(x_inter, dy_inter), bias_grad(dy_inter),
              weight_grad(x_out, dy_out), bias_grad(dy_out), ln_rows[2], ln_rows[3]]
    filled_len = sum(grad_piece.size for grad_piece in pieces)
    pieces.append(jnp.zeros((total_len - filled_len,), jnp.float32))
    return jnp.concatenate([grad_piece.reshape(-1) for grad_piece in pieces])


def adam_direction(grad_hat, weights, moment_one, moment_two, seg_ids):
    new_m = BETA_ONE * moment_one + (1.0 - BETA_ONE) * grad_hat
    new_v = BETA_TWO * moment_two + (1.0 - BETA_TWO) * grad_hat * grad_hat
    decay_mask = ((seg_ids == 0) | (seg_ids == 2) | (seg_ids == 6) | (seg_ids == 8)).astype(jnp.float32)
    update = (new_m / CORR_ONE) / (jnp.sqrt(new_v / CORR_TWO) + EPSILON) + DECAY * decay_mask * weights
    return new_m, new_v, update


def trust_ratio(w_sq, u_sq):
    w_norm = jnp.sqrt(w_sq)
    u_norm = jnp.sqrt(u_sq)
    both_pos = (w_norm > 0) & (u_norm > 0)
    return jnp.where(both_pos, w_norm / jnp.where(u_norm > 0, u_norm, 1.0), 1.0)


def solution(mesh):
    axis_size = mesh.shape['dp']

    def local_step(weights, moment_one, moment_two, x_qkv, dy_qkv, x_proj, dy_proj, x_inter, dy_inter, x_out, dy_out, ln_grad):
        layer_width = x_qkv.shape[1]
        shard_len = weights.shape[0]
        act_pairs = (x_qkv, dy_qkv, x_proj, dy_proj, x_inter, dy_inter, x_out, dy_out)
        local_grad = flat_grad(act_pairs, ln_grad[0], shard_len * axis_size)
        mean_grad = lax.psum_scatter(local_grad, 'dp', scatter_dimension=0, tiled=True) / axis_size
        grad_norm = jnp.sqrt(lax.psum(jnp.sum(mean_grad * mean_grad), 'dp'))
        grad_hat = mean_grad / jnp.maximum(1.0, grad_norm)
        positions = lax.axis_index('dp') * shard_len + lax.iota(jnp.int32, shard_len)
        seg_ids = segment_index(positions, layer_width)
        new_m, new_v, update = adam_direction(grad_hat, weights, moment_one, moment_two, seg_ids)
        part_sums = jnp.stack([tensor_sums(weights * weights, seg_ids), tensor_sums(update * update, seg_ids)])
        total_sums = lax.psum(part_sums, 'dp')
        trust_vec = trust_ratio(total_sums[0], total_sums[1])
        new_w = weights - LEARN_RATE * per_element(trust_vec, seg_ids) * update
        full_w = lax.optimization_barrier(lax.all_gather(new_w, 'dp', axis=0, tiled=True))
        params = full_w.astype(jnp.bfloat16)
        return new_w, new_m, new_v, params

    row_spec = P('dp', None)
    in_specs = (P('dp'), P('dp'), P('dp'), row_spec, row_spec, row_spec, row_spec, row_spec, row_spec, row_spec, row_spec, P('dp', None, None))
    out_specs = (P('dp'), P('dp'), P('dp'), P())
    return jax.shard_map(local_step, mesh=mesh, in_specs=in_specs, out_specs=out_specs, check_vma=False)
```

profile of v0, /device:TPU:0, one launch (start us, length us, event | category | flops | bytes accessed | tf_op | source)
XLA Modules:
  0.0 347.9 jit_solution(16642633402106442736)
XLA Ops:
  7.2 0.0 copy-start
  7.2 0.0 all-reduce.3.cloned.1.call-start
  7.2 0.0 copy-start.2
  7.2 0.9 fusion.18
  8.1 4.0 %convert_reduce_fusion.1 = f32[768]{0:T(1024)S(1)} fusion(bf16[4096,768]{1,0:T(8,128)(2,1)} %param.16), kind=kLoop, calls=%fused_computation.1 | loop fusion | flops 6290688 | bytes 6294528 | tf_op jit(solution)/shard_map/reduce_sum | solution.py:47
  12.1 3.4 fusion.19
  15.6 0.9 reshape.87
  16.5 2.2 constant_dynamic-update-slice_fusion.12
  18.7 2.8 convert_reduce_fusion.3
  21.5 3.0 convolution_bitcast_fusion.2
  24.5 0.1 copy.16
  24.7 0.0 slice-start
  24.7 1.2 convert_reduce_fusion
  25.9 0.0 slice-start.1
  26.0 2.3 convolution_bitcast_fusion.1
  28.3 0.2 copy.17
  28.5 1.4 copy-done.3
  29.9 0.6 convert_reduce_fusion.2
  30.5 2.4 convolution_bitcast_fusion
  32.8 0.5 copy.18
  33.4 1.3 constant_dynamic-update-slice_fusion.11
  34.7 1.7 constant_dynamic-update-slice_fusion.10
  36.4 1.3 constant_dynamic-update-slice_fusion.9
  37.7 1.3 constant_dynamic-update-slice_fusion.8
  39.0 1.3 constant_dynamic-update-slice_fusion.7
  40.2 2.3 constant_dynamic-update-slice_fusion.6
  42.6 1.3 constant_dynamic-update-slice_fusion.5
  43.9 2.3 constant_dynamic-update-slice_fusion.4
  46.3 1.3 constant_dynamic-update-slice_fusion.3
  47.6 1.3 constant_dynamic-update-slice_fusion.2
  48.9 1.3 constant_dynamic-update-slice_fusion.1
  50.1 1.3 constant_dynamic-update-slice_fusion
  51.4 0.0 all-reduce.3.cloned.1.call-update
  51.4 0.0 all-gather.3.cloned.1.call-start
  51.5 140.6 %all-reduce.3.cloned.1.call-done = f32[790528]{0:T(1024)} async-done(((f32[790528]{0:T(1024)}), f32[790528]{0:T(1024)}) %all-reduce.3.cloned.1.call-update) | async-done | bytes 3162128
  192.1 1.6 multiply_reduce_fusion
  193.7 0.1 convert_add_fusion
  193.8 40.6 %psum.14 = f32[]{:T(128)} all-reduce(f32[]{:T(128)} %multiply_reduce_fusion), channel_id=1, replica_groups=mesh['dp'=32] {'dp'}, use_global_device_ids=true, to_apply=%region_7.8 | all-reduce | flops 1 | bytes 8 | tf_op jit(solution)/shard_map/psum | solution.py:84
  235.2 1.2 fusion.16
  236.3 0.7 select_reduce_fusion.2
  237.1 39.5 %psum.15 = f32[2,13]{1,0:T(2,128)S(1)} all-reduce(f32[2,13]{1,0:T(2,128)S(1)} %pad_maximum_fusion), channel_id=1, replica_groups=mesh['dp'=32] {'dp'}, use_global_device_ids=true, to_apply=%region_9.10 | all-reduce | flops 26 | bytes 208 | tf_op jit(solution)/shard_map/psum | solution.py:90
  276.6 0.5 select_reduce_fusion
  277.1 0.2 multiply_subtract_fusion
  277.3 0.0 copy-start.4
  277.3 0.7 reshape.91
  278.0 0.0 all-gather.3.cloned.1.call-update
  278.1 59.8 %all-gather.3.cloned.1.call-done = f32[32,1,24704]{2,1,0:T(1,128)} async-done(((f32[1,1,24704]{2,1,0:T(1,128)}), f32[32,1,24704]{2,1,0:T(1,128)}) %all-gather.3.cloned.1.call-update) | async-done | bytes 3162128 | tf_op jit(solution)/shard_map/all_gather | solution.py:93
  337.9 3.2 convert_element_type.116
  (21 shorter events, 0.1 us)
Async XLA Ops:
  7.2 18.8 %copy-start = (bf16[4096,256]{1,0:T(8,128)(2,1)S(1)}, bf16[4096,256]{1,0:T(8,128)(2,1)}, u32[]{:S(2)}) copy-start(bf16[4096,256]{1,0:T(8,128)(2,1)} %param.19) | copy-start | bytes 6291460
  7.2 184.9 %all-reduce.3.cloned.1.call-start = ((), (), s32[]{:S(2)}) async-start(), calls=%async_computation.1 | async-start | bytes 6324224
  7.2 4.9 %copy-start.2 = (bf16[4096,768]{1,0:T(8,128)(2,1)S(1)}, bf16[4096,768]{1,0:T(8,128)(2,1)}, u32[]{:S(2)}) copy-start(bf16[4096,768]{1,0:T(8,128)(2,1)} %param.16) | copy-start | bytes 18874372
  16.5 8.2 %copy-start.1 = (bf16[4096,1024]{1,0:T(8,128)(2,1)S(1)}, bf16[4096,1024]{1,0:T(8,128)(2,1)}, u32[]{:S(2)}) copy-start(bf16[4096,1024]{1,0:T(8,128)(2,1)} %param.20) | copy-start | bytes 25165828
  24.7 5.8 %slice-start = ((s8[8388608]{0:T(1024)(128)(4,1)}), s8[4194304]{0:T(1024)(128)(4,1)S(1)}, s32[]{:S(2)}) async-start(s8[8388608]{0:T(1024)(128)(4,1)} %bitcast.28), calls=%async_computation.2 | async-start | bytes 8388608
  25.9 4.5 %slice-start.1 = ((s8[8388608]{0:T(1024)(128)(4,1)}), s8[4194304]{0:T(1024)(128)(4,1)S(1)}, s32[]{:S(2)}) async-start(s8[8388608]{0:T(1024)(128)(4,1)} %bitcast.28), calls=%async_computation.3 | async-start | bytes 8388608
  28.3 1.6 copy-start.3
  42.6 192.6 %copy-start.5 = (f32[24704]{0:T(1024)S(1)}, f32[24704]{0:T(1024)}, u32[]{:S(2)}) copy-start(f32[24704]{0:T(1024)} %param.12) | copy-start | bytes 296452
  42.6 192.6 %copy-start.8 = (f32[24704]{0:T(1024)S(1)}, f32[24704]{0:T(1024)}, u32[]{:S(2)}) copy-start(f32[24704]{0:T(1024)} %param.13) | copy-start | bytes 296452
  42.6 192.6 %copy-start.9 = (f32[24704]{0:T(1024)S(1)}, f32[24704]{0:T(1024)}, u32[]{:S(2)}) copy-start(f32[24704]{0:T(1024)} %param.14) | copy-start | bytes 296452
  51.4 286.4 %all-gather.3.cloned.1.call-start = ((), (), s32[]{:S(2)}) async-start(), calls=%async_computation | async-start | bytes 3260928 | tf_op jit(solution)/shard_map/all_gather | solution.py:93
  236.3 104.8 %copy-start.6 = (f32[24704]{0:T(1024)}, f32[24704]{0:T(1024)S(1)}, u32[]{:S(2)}) copy-start(f32[24704]{0:T(1024)S(1)} %get-tuple-element.7) | copy-start | bytes 296452
  236.3 104.7 %copy-start.7 = (f32[24704]{0:T(1024)}, f32[24704]{0:T(1024)S(1)}, u32[]{:S(2)}) copy-start(f32[24704]{0:T(1024)S(1)} %get-tuple-element.8) | copy-start | bytes 296452
  277.3 63.8 %copy-start.4 = (f32[24704]{0:T(1024)}, f32[24704]{0:T(1024)S(1)}, u32[]{:S(2)}) copy-start(f32[24704]{0:T(1024)S(1)} %multiply_subtract_fusion) | copy-start | bytes 296452
Sparse Core Ops, SparseCore 0:
  51.6 140.4 all-reduce.2
  278.2 59.6 all-gather.2
where the time goes:
time: 349 us; the launch traced here: 348 us
  waiting for transfers between devices  200 us (57%)
  blocking collectives  80.1 us (23%)
  local copies, waits for them, and re-layouts  25.1 us (7%)
  other arithmetic  16.2 us (5%)
  between operations  15 us (4%)
  matrix products  11.1 us (3%)
    unnamed x3, waiting for transfers between devices  141 us
    all_gather x1, waiting for transfers between devices, local_step(): lax.all_gather(new_w, 'dp', axis=0, tiled=True)  59.8 us
    psum x1, blocking collectives, local_step(): grad_norm = jnp.sqrt(lax.psum(jnp.sum(mean_grad * mean_grad), 'dp'))  40.6 us
    psum x1, blocking collectives, local_step(): total_sums = lax.psum(part_sums, 'dp')  39.5 us
    unnamed x40, local copies, waits for them, and re-layouts  22 us
    dot_general x4, matrix products, weight_grad(): lax.dot_general(x_rows, dy_rows, CONTRACT_ROWS, preferred_element_type=jn...  11.1 us
    reduce_sum x4, other arithmetic, bias_grad(): return jnp.sum(dy_rows, axis=0, dtype=jnp.float32)  8.63 us
  transfers between devices with their start and end apart: 2, of which 2 were waited for; matrix products, arithmetic and copies ran while one was open for 0% of the time, Pallas kernels for 0%

commit v1 on v0

v1 whole, which is shorter than its diff:
```python
import functools

import jax
import jax.numpy as jnp
from jax import lax
from jax.experimental import pallas as pl
from jax.experimental.pallas import tpu as pltpu
from jax.sharding import PartitionSpec as P

STEP = 10
LEARN_RATE = 0.5
BETA_ONE = 0.9
BETA_TWO = 0.999
EPSILON = 1e-6
DECAY = 0.01
CORR_ONE = 1.0 - BETA_ONE ** STEP
CORR_TWO = 1.0 - BETA_TWO ** STEP

LANES = 128
CHUNKS = 4
PARTS = 4
F32 = jnp.float32
BF16 = jnp.bfloat16


def tensor_sizes(width):
    return [3 * width * width, 3 * width, width * width, width, width, width,
            4 * width * width, 4 * width, 4 * width * width, width, width, width]


def row_ends(width):
    ends, total = [], 0
    for size in tensor_sizes(width):
        total += size // LANES
        ends.append(total)
    return ends


def comm_kernel(dims, x_qkv, dy_qkv, x_proj, dy_proj, x_inter, dy_inter, x_out, dy_out, ln, w_in, m_in, v_in,
                nw_out, nm_out, nv_out, par_out,
                bx_qkv, by_qkv, bx_proj, by_proj, bx_inter, by_inter, bx_out, by_out, ln_v, w_v, m_v, v_v,
                nw_v, nm_v, nv_v, acc, gflat, r_d, r_1, r_2, r_z, stat1, stat2, wfull, pbf,
                in_sem, st_sem, out_sem, sd_s, sd_r, s1_s, s1_r, s2_s, s2_r, sz_s, sz_r,
                t1_s, t1_r, t2_s, t2_r, ag_s, ag_r):
    width, shard, ndev, rows = dims
    tokens = x_qkv.shape[0]
    step = tokens // CHUNKS
    ends = row_ends(width)
    me = lax.axis_index('dp')
    core, xx, yy, zz = me % 2, (me // 2) % 2, (me // 4) % 2, me // 8
    partner = me + 1 - 2 * core
    first = xx * (1 - core) + yy * core
    second = yy * (1 - core) + xx * core
    peer1 = me + (1 - 2 * first) * (2 * (1 - core) + 4 * core)
    peer2 = me + (1 - 2 * second) * (4 * (1 - core) + 2 * core)

    def slot(a, b):
        return (1 - core) * (2 * b + a) + core * (2 * a + b)

    pairs = [(x_out, bx_out, dy_out, by_out), (x_inter, bx_inter, dy_inter, by_inter),
             (x_proj, bx_proj, dy_proj, by_proj), (x_qkv, bx_qkv, dy_qkv, by_qkv)]
    loads = {}
    for p, (xs, xd, ys, yd) in enumerate(pairs):
        for k in range(CHUNKS):
            at = pl.ds(k * step, step)
            for q, (src, dst) in enumerate(((xs, xd), (ys, yd))):
                copy = pltpu.make_async_copy(src.at[at], dst.at[at], in_sem.at[p, k, q])
                copy.start()
                loads[p, k, q] = copy
    small = [pltpu.make_async_copy(s, d, st_sem.at[i])
             for i, (s, d) in enumerate(((ln, ln_v), (w_in, w_v), (m_in, m_v), (v_in, v_v)))]
    for copy in small:
        copy.start()

    barrier = pltpu.get_barrier_semaphore()
    for i in range(1, ndev):
        pl.semaphore_signal(barrier, inc=1, device_id=((me + i) % ndev,), device_id_type=pl.DeviceIdType.MESH)

    def remote(src, dst, s_sem, r_sem, dev):
        return pltpu.make_async_remote_copy(src_ref=src, dst_ref=dst, send_sem=s_sem, recv_sem=r_sem,
                                            device_id=(dev,), device_id_type=pl.DeviceIdType.MESH)

    ones = jnp.ones((16, step), BF16)

    def matmul(p, xb, yb, n):
        for k in range(CHUNKS):
            loads[p, k, 0].wait()
            loads[p, k, 1].wait()
            at = pl.ds(k * step, step)
            lhs = jnp.concatenate([xb[at, :].T, ones], axis=0)
            part = jnp.dot(lhs, yb[at, :], preferred_element_type=F32)
            if k == 0:
                acc[:, :n] = part
            else:
                acc[:, :n] += part

    def spread(base, n):
        cols = n // LANES
        for j in range(cols):
            gflat[pl.ds(base + j, width, stride=cols), :] = acc[0:width, j * LANES:(j + 1) * LANES]
            gflat[pl.ds(base + cols * width + j, 1), :] = acc[width:width + 1, j * LANES:(j + 1) * LANES]

    def matmul_out():
        cols = width // LANES
        inner = x_out.shape[1]
        for k in range(CHUNKS):
            loads[0, k, 0].wait()
            loads[0, k, 1].wait()
            at = pl.ds(k * step, step)
            y = by_out[at, :]
            part = jnp.dot(y.T, bx_out[at, :], preferred_element_type=F32)
            bias = jnp.dot(ones, y, preferred_element_type=F32)[0:8]
            if k == 0:
                acc[0:width, :] = part
                acc[width:width + 8, 0:width] = bias
            else:
                acc[0:width, :] += part
                acc[width:width + 8, 0:width] += bias
        base = ends[7]
        for j in range(cols):
            gflat[pl.ds(base + j, inner, stride=cols), :] = acc[j * LANES:(j + 1) * LANES, :].T
            gflat[pl.ds(ends[8] + j, 1), :] = acc[width:width + 1, j * LANES:(j + 1) * LANES]

    def send_d(g):
        for q in range(4):
            s = g * 8 + q * 2 + 1 - core
            remote(gflat.at[pl.ds(s * shard, shard)], r_d.at[g * 4 + q, pl.ds(0, shard)],
                   sd_s.at[g * 4 + q], sd_r.at[g * 4 + q], partner).start()

    def copy_1(g, b):
        return remote(r_d.at[g * 4 + slot(1 - first, b), pl.ds(0, shard)], r_1.at[g * 2 + b, pl.ds(0, shard)],
                      s1_s.at[g * 2 + b], s1_r.at[g * 2 + b], peer1)

    def copy_2(g):
        return remote(r_1.at[g * 2 + 1 - second, pl.ds(0, shard)], r_2.at[g, pl.ds(0, shard)],
                      s2_s.at[g], s2_r.at[g], peer2)

    def recv_d(j, a, b, g):
        q = slot(a, b)
        i = g * 4 + q
        remote(gflat.at[pl.ds(0, shard)], r_d.at[i, pl.ds(0, shard)], sd_s.at[i], sd_r.at[i], partner).wait_recv()
        r_d[i, 0:shard, :] += gflat[pl.ds((g * 8 + q * 2 + core) * shard, shard), :]

    def d_to_1(g):
        for b in range(2):
            recv_d(0, 1 - first, b, g)
            copy_1(g, b).start()
        for b in range(2):
            recv_d(0, first, b, g)

    def one_to_2(g):
        for b in (1 - second, second):
            i = g * 2 + b
            remote(r_d.at[0, pl.ds(0, shard)], r_1.at[i, pl.ds(0, shard)], s1_s.at[i], s1_r.at[i], peer1).wait_recv()
            r_1[i, 0:shard, :] += r_d[g * 4 + slot(first, b), 0:shard, :]
            if b is not second:
                copy_2(g).start()

    def two_to_z(g):
        copy_2(g).wait_recv()
        r_2[g, 0:shard, :] += r_1[g * 2 + second, 0:shard, :]

        @pl.when(zz != g)
        def _():
            remote(r_2.at[g, pl.ds(0, shard)], r_z.at[zz, pl.ds(0, shard)], sz_s.at[g], sz_r.at[zz],
                   me + (g - zz) * 8).start()

    matmul_out()
    small[0].wait()
    half = 2 * width // LANES
    gflat[pl.ds(ends[3], half), :] = ln_v[0:half, :]
    gflat[pl.ds(ends[9], half), :] = ln_v[half:2 * half, :]
    gflat[pl.ds(ends[11], rows - ends[11]), :] = jnp.zeros((rows - ends[11], LANES), F32)
    pl.semaphore_wait(barrier, ndev - 1)
    send_d(3)
    matmul(1, bx_inter, by_inter, 4 * width)
    spread(ends[5], 4 * width)
    d_to_1(3)
    send_d(2)
    matmul(2, bx_proj, by_proj, width)
    spread(ends[1], width)
    one_to_2(3)
    d_to_1(2)
    send_d(1)
    matmul(3, bx_qkv, by_qkv, 3 * width)
    spread(0, 3 * width)
    send_d(0)
    two_to_z(3)
    one_to_2(2)
    d_to_1(1)
    d_to_1(0)
    two_to_z(2)
    one_to_2(1)
    one_to_2(0)
    two_to_z(1)
    two_to_z(0)

    for copy in small[1:]:
        copy.wait()
    lane = lax.broadcasted_iota(jnp.int32, (shard, LANES), 1)
    row = lax.broadcasted_iota(jnp.int32, (shard, LANES), 0) + me * shard
    seg = jnp.zeros((shard, LANES), jnp.int32)
    for end in ends:
        seg = seg + jnp.where(row >= end, 1, 0)
    mine = lane == seg
    w = w_v[...]

    def seg_sums(val):
        per_row = jnp.sum(val, axis=1, keepdims=True)
        return jnp.sum(jnp.where(mine, per_row, 0.0), axis=0, keepdims=True)

    w_sums = seg_sums(w * w)

    g = r_2[zz, 0:shard, :]
    for d in range(1, PARTS):
        src = (zz + d) % PARTS
        remote(r_2.at[0, pl.ds(0, shard)], r_z.at[src, pl.ds(0, shard)], sz_s.at[0], sz_r.at[src], me).wait_recv()
        g = g + r_z[src, 0:shard, :]
    g = g * (1.0 / ndev)

    def exchange(stat, value, s_sem, r_sem):
        stat[pl.ds(me, 1), :] = value
        for i in range(1, ndev):
            remote(stat.at[pl.ds(me, 1)], stat.at[pl.ds(me, 1)], s_sem.at[i], r_sem, (me + i) % ndev).start()
        pltpu.make_async_copy(stat.at[pl.ds(0, ndev - 1)], stat.at[pl.ds(0, ndev - 1)], r_sem).wait()
        return jnp.sum(stat[...], axis=0, keepdims=True)

    one_lane = lax.broadcasted_iota(jnp.int32, (1, LANES), 1)
    g_sq = jnp.sum(jnp.sum(g * g, axis=0, keepdims=True), axis=1, keepdims=True)
    total1 = exchange(stat1, jnp.where(one_lane == 64, g_sq, w_sums), t1_s, t1_r)
    gn = jnp.sqrt(jnp.sum(jnp.where(one_lane == 64, total1, 0.0), axis=1, keepdims=True))
    h = g / jnp.maximum(1.0, gn)
    new_m = BETA_ONE * m_v[...] + (1.0 - BETA_ONE) * h
    new_v = BETA_TWO * v_v[...] + (1.0 - BETA_TWO) * h * h
    decay = jnp.where((seg == 0) | (seg == 2) | (seg == 6) | (seg == 8), DECAY, 0.0)
    u = (new_m / CORR_ONE) / (jnp.sqrt(new_v / CORR_TWO) + EPSILON) + decay * w
    total2 = exchange(stat2, seg_sums(u * u), t2_s, t2_r)
    nm_v[...] = new_m
    nv_v[...] = new_v
    w_norm, u_norm = jnp.sqrt(total1), jnp.sqrt(total2)
    ratio = jnp.where((w_norm > 0) & (u_norm > 0), w_norm / jnp.where(u_norm > 0, u_norm, 1.0), 1.0)
    per_row = jnp.sum(jnp.where(mine, ratio, 0.0), axis=1, keepdims=True)
    new_w = w - LEARN_RATE * per_row * u
    nw_v[...] = new_w
    wfull[pl.ds(me * shard, shard), :] = new_w
    outs = [pltpu.make_async_copy(s, d, out_sem.at[i])
            for i, (s, d) in enumerate(((nw_v, nw_out), (nm_v, nm_out), (nv_v, nv_out)))]

    def shard_at(s):
        return wfull.at[pl.ds(s * shard, shard)]

    sent = []

    def push(s, dev, src=None):
        copy = remote(shard_at(s) if src is None else src, shard_at(s), ag_s.at[len(sent)], ag_r.at[s], dev)
        copy.start()
        sent.append(copy)

    def arrived(s):
        remote(shard_at(s), shard_at(s), ag_s.at[0], ag_r.at[s], me).wait_recv()

    zs = [zz, zz + 1 - 2 * (zz % 2), 3 - zz, zz + 2 - 4 * (zz // 2)]

    def shifted(s, j):
        return s + (zs[j] - zz) * 8

    push(me, peer2, nw_v)
    push(me, peer1, nw_v)
    for j in range(1, PARTS):
        push(me, shifted(me, j), nw_v)
    push(me, partner, nw_v)
    for copy in outs:
        copy.start()
    diag = peer1 + peer2 - me
    for j in range(PARTS):
        if j:
            arrived(shifted(me, j))
            for dev in (peer2, peer1, partner):
                push(shifted(me, j), dev)
        s = shifted(peer1, j)
        arrived(s)
        push(s, peer2)
        push(s, partner)
    for j in range(PARTS):
        for base in (peer2, diag):
            s = shifted(base, j)
            arrived(s)
            push(s, partner)
    other = partner - core + (1 - core)
    for k in range(ndev // 2):
        arrived(2 * k + 1 - core)
    block = rows // PARTS
    half_rows = [i * rows // 2 for i in range(3)]
    par = []
    for i in range(2):
        at = pl.ds(half_rows[i], rows // 2)
        pbf[at, :] = wfull[at, :].astype(BF16)
        copy = pltpu.make_async_copy(pbf.at[at], par_out.at[at], out_sem.at[3 + i])
        copy.start()
        par.append(copy)

    for g_ in range(PARTS):
        for q in range(4):
            i = g_ * 4 + q
            remote(gflat.at[pl.ds(0, shard)], r_d.at[i, pl.ds(0, shard)], sd_s.at[i], sd_r.at[i], partner).wait_send()
        for b in range(2):
            copy_1(g_, b).wait_send()
        copy_2(g_).wait_send()

        @pl.when(zz != g_)
        def _():
            remote(r_2.at[g_, pl.ds(0, shard)], r_z.at[0, pl.ds(0, shard)], sz_s.at[g_], sz_r.at[0], me).wait_send()
    for i in range(1, ndev):
        for stat, sem, rs in ((stat1, t1_s, t1_r), (stat2, t2_s, t2_r)):
            remote(stat.at[pl.ds(0, 1)], stat.at[pl.ds(0, 1)], sem.at[i], rs, me).wait_send()
    for copy in sent:
        copy.wait_send()
    for copy in outs + par:
        copy.wait()


def solution(mesh):
    ndev = mesh.shape['dp']

    def local_step(weights, moment_one, moment_two, x_qkv, dy_qkv, x_proj, dy_proj, x_inter, dy_inter, x_out, dy_out, ln_grad):
        width = x_qkv.shape[1]
        shard = weights.shape[0] // LANES
        rows = shard * ndev
        flat = lambda a: a.reshape(-1, LANES)
        acts = (x_qkv, dy_qkv, x_proj, dy_proj, x_inter, dy_inter, x_out, dy_out)
        vm = pltpu.VMEM
        pad = -(-shard // 8) * 8
        state = jax.ShapeDtypeStruct((shard, LANES), F32)
        dma = pltpu.SemaphoreType.DMA
        hbm = pl.BlockSpec(memory_space=pl.ANY)
        outs = pl.pallas_call(
            functools.partial(comm_kernel, (width, shard, ndev, rows)),
            out_shape=(state, state, state, jax.ShapeDtypeStruct((rows, LANES), BF16)),
            in_specs=[hbm] * 12,
            out_specs=(hbm,) * 4,
            scratch_shapes=[vm(a.shape, BF16) for a in acts] + [
                vm((4 * width // LANES, LANES), F32)] + [vm((shard, LANES), F32)] * 6 + [
                vm((width + 16, 4 * width), F32), vm((rows, LANES), F32),
                vm((16, pad, LANES), F32), vm((8, pad, LANES), F32), vm((4, pad, LANES), F32), vm((4, pad, LANES), F32),
                vm((ndev, LANES), F32), vm((ndev, LANES), F32), vm((rows, LANES), F32), vm((rows, LANES), BF16),
                dma((4, CHUNKS, 2)), dma((4,)), dma((5,)), dma((16,)), dma((16,)), dma((8,)), dma((8,)),
                dma((4,)), dma((4,)), dma((4,)), dma((4,)),
                dma((ndev,)), dma, dma((ndev,)), dma, dma((40,)), dma((ndev,))],
            compiler_params=pltpu.CompilerParams(collective_id=0, has_side_effects=True, vmem_limit_bytes=60 * 2 ** 20),
            name='lamb_step',
        )(*acts, flat(ln_grad), flat(weights), flat(moment_one), flat(moment_two))
        new_w, new_m, new_v, params = outs
        return new_w.reshape(-1), new_m.reshape(-1), new_v.reshape(-1), params.reshape(-1)

    row_spec = P('dp', None)
    in_specs = (P('dp'), P('dp'), P('dp'), row_spec, row_spec, row_spec, row_spec, row_spec, row_spec, row_spec, row_spec, P('dp', None, None))
    out_specs = (P('dp'), P('dp'), P('dp'), P())
    return jax.shard_map(local_step, mesh=mesh, in_specs=in_specs, out_specs=out_specs, check_vma=False)
```

time: 349 us -> 91.2 us (0.26)
  waiting for transfers between devices: 200 us -> 0 us
  Pallas kernels: 0 us -> 81 us
  blocking collectives: 80.1 us -> 0 us
  local copies, waits for them, and re-layouts: 25.1 us -> 8.57 us
  other arithmetic: 16.2 us -> 0 us
  between operations: 15 us -> 0.64 us
  matrix products: 11.1 us -> 0 us
    unnamed x3 -> x0, waiting for transfers between devices: 141 us -> none
    pallas_call x0 -> x1, Pallas kernels: none -> 81 us  [local_step(): pl.pallas_call(functools.partial(comm_kernel, (width, shard, ndev, rows))...]
    psum x2 -> x0, blocking collectives: 80.1 us -> none  [the longest x1 40.6 us: local_step(): grad_norm = jnp.sqrt(lax.psum(jnp.sum(mean_grad * mean_grad), 'dp'))]
    all_gather x1 -> x0, waiting for transfers between devices: 59.8 us -> none  [local_step(): lax.all_gather(new_w, 'dp', axis=0, tiled=True)]
    unnamed x40 -> x4, local copies, waits for them, and re-layouts: 22 us -> 7.28 us
    reduce_sum x7 -> x0, other arithmetic: 11.5 us -> none  [the longest x4 8.63 us: bias_grad(): return jnp.sum(dy_rows, axis=0, dtype=jnp.float32)]
    dot_general x4 -> x0, matrix products: 11.1 us -> none  [weight_grad(): lax.dot_general(x_rows, dy_rows, CONTRACT_ROWS, preferred_element_type=jn...]
  transfers between devices with their start and end apart: 2 -> 0, of which waited for: 2 -> 0; matrix products, arithmetic and copies ran while one was open for 0% -> 0% of each run, Pallas kernels for 0% -> 0%
where the time goes in v1:
time: 91.2 us; the launch traced here: 90.2 us
  Pallas kernels  81 us (89%)
  local copies, waits for them, and re-layouts  8.57 us (9%)
    pallas_call x1, Pallas kernels, local_step(): pl.pallas_call(functools.partial(comm_kernel, (width, shard, ndev, rows))...  81 us
    unnamed x4, local copies, waits for them, and re-layouts  7.28 us

profile of v1, /device:TPU:0, one launch (start us, length us, event | category | flops | bytes accessed | tf_op | source)
XLA Modules:
  0.0 90.2 jit_solution(14780939562117569999)
XLA Ops:
  0.6 1.3 %reshape.32.ln = f32[8,128]{1,0:T(8,128)} reshape(f32[1,4,256]{2,1,0:T(4,128)} %param.23) | data formatting | bytes 8192 | tf_op jit(solution)/shard_map/reshape | solution.py:329
  1.9 81.0 %lamb_step.1 = (f32[193,128]{1,0:T(8,128)}, f32[193,128]{1,0:T(8,128)}, f32[193,128]{1,0:T(8,128)}, bf16[6176,128]{1,0:T(8,128)(2,1)}) custom-call(bf16[4096,256]{1,0:T(8,128)(2,1)} %x_qkv.1, bf16[4096,768]{1,0:T(8,128)(2,1)} %dy_qkv.1, bf16[4096,256]{1,0:T(8,128)(2,1)} %x_proj.1, bf16[4096,256]{1,0:T(8,128)(2,1)} %dy_proj.1, bf16[4096,256]{1,0:T(8,128)(2,1)} %x_inter.1, ...), custom_call_target="tpu_custom_call" | custom-call | tf_op jit(solution)/shard_map/lamb_step/pallas_call | solution.py:336
  82.9 1.5 %copy.20 = f32[24704]{0:T(1024)} copy(f32[24704]{0:T(1024)} %bitcast.13) | data formatting | bytes 197632
  84.4 1.5 %copy.21 = f32[24704]{0:T(1024)} copy(f32[24704]{0:T(1024)} %bitcast.12) | data formatting | bytes 197632
  86.0 1.5 %copy.22 = f32[24704]{0:T(1024)} copy(f32[24704]{0:T(1024)} %bitcast.11) | data formatting | bytes 197632
  87.5 2.7 %copy.23 = bf16[790528]{0:T(1024)(128)(2,1)} copy(bf16[790528]{0:T(1024)(128)(2,1)} %bitcast.7) | data formatting | bytes 3162112
